TPU v7x, 32 devices: a whole 2x2x4 slice. The times are simulated.
32 devices in a mesh: seq: 16 (over z, x, core), head: 2 (over y).
Axes of the slice: x: 2, y: 2, z: 4, core: 2. Of those that a mesh axis runs over, the one named last changes fastest.
Arguments:
- query: bfloat16 [8192, 1024], P('seq', 'head'), may hold values from -6 to 6
- key_rows: bfloat16 [8192, 128], P('seq'), may hold values from -6 to 6
- value_rows: bfloat16 [8192, 128], P('seq'), may hold values from -6 to 6
- output: bfloat16 [8192, 1024], P('seq', 'head'), may hold values from -1.5 to 1.5
- grad_output: bfloat16 [8192, 1024], P('seq', 'head'), may hold values from -144 to 144
- log_norm: float32 [8, 8192], P('head', 'seq'), may hold values from 0.5 to 12
- stripe: int32 [16], replicated, may hold values from 0 to 15, each once
Outputs:
- grad_query: bfloat16 [8192, 1024], P('seq', 'head')
- grad_key: bfloat16 [8192, 128], P(('seq', 'head'))
- grad_value: bfloat16 [8192, 128], P(('seq', 'head'))
Inputs may be any that keep to these rules, and one draw needn't show every extreme that they name: stripe is a permutation of 0 to 15.
All inputs are finite; a program needn't handle non-finite values.
Results may differ from a plain program's by a relative error of at most 0.0051.
Values may be sent and summed in bfloat16 or wider, within the bound.
A program may use at most 192 MiB of HBM per device.

v0:
```python
import jax
import jax.numpy as jnp
from jax import lax
from jax.sharding import PartitionSpec as P

WINDOW = 8


def from_behind(block, axis, distance):
    devices = range(lax.axis_size(axis))
    route = [((i - distance) % len(devices), i) for i in devices]
    return lax.ppermute(block, axis, route)


def block_terms(query_heads, grad_heads, lse_rows, delta_rows, kv_pair, diag_open):
    key_block = kv_pair[0]
    value_block = kv_pair[1]
    extent = key_block.shape[0]
    factor = key_block.shape[1] ** (-0.5)
    scores = (
        jnp.einsum("shd,td->hst", query_heads, key_block, preferred_element_type=jnp.float32)
        * factor
    )
    row_ids = lax.broadcasted_iota(jnp.int32, (extent, extent), 0)
    col_ids = lax.broadcasted_iota(jnp.int32, (extent, extent), 1)
    allowed = (col_ids < row_ids) | (col_ids == row_ids) & diag_open
    weights = jnp.where(allowed[None], jnp.exp(scores - lse_rows[:, :, None]), 0.0)
    weights_low = weights.astype(jnp.bfloat16)
    grad_values = jnp.einsum(
        "hst,shd->td", weights_low, grad_heads, preferred_element_type=jnp.float32
    )
    grad_weights = jnp.einsum(
        "shd,td->hst", grad_heads, value_block, preferred_element_type=jnp.float32
    )
    grad_scores = (factor * weights * (grad_weights - delta_rows[:, :, None])).astype(jnp.bfloat16)
    grad_query = jnp.einsum(
        "hst,td->shd", grad_scores, key_block, preferred_element_type=jnp.float32
    )
    grad_keys = jnp.einsum(
        "hst,shd->td", grad_scores, query_heads, preferred_element_type=jnp.float32
    )
    return (grad_query, jnp.stack([grad_keys, grad_values]))


def stripe_at(stripe, where_index):
    slot_ids = lax.broadcasted_iota(jnp.int32, stripe.shape, 0)
    return jnp.sum(jnp.where(slot_ids == where_index, stripe, 0))


def shards(query, key_rows, value_rows, output, grad_output, log_norm, stripe):
    extent = query.shape[0]
    head_dim = key_rows.shape[1]
    local_heads = query.shape[1] // head_dim
    query_heads = query.reshape(extent, local_heads, head_dim)
    grad_heads = grad_output.reshape(extent, local_heads, head_dim)
    output_heads = output.reshape(extent, local_heads, head_dim)
    delta_rows = jnp.sum(
        grad_heads.astype(jnp.float32) * output_heads.astype(jnp.float32), axis=2
    ).T
    cycle_length = lax.axis_size("seq")
    cycle_index = lax.axis_index("seq")
    own_stripe = stripe_at(stripe, cycle_index)

    def compute(kv_pair, offset):
        source = (cycle_index - offset) % cycle_length
        diag_open = stripe_at(stripe, source) <= own_stripe
        query_part, key_part = block_terms(
            query_heads, grad_heads, log_norm, delta_rows, kv_pair, diag_open
        )
        return (query_part, key_part)

    kv_pair = jnp.stack([key_rows, value_rows])
    grad_query, own_part = compute(kv_pair, 0)
    kv_pair = from_behind(kv_pair, "seq", WINDOW - 1)
    carried = jnp.zeros_like(own_part)
    for offset in range(WINDOW - 1, 0, -1):
        query_part, key_part = compute(kv_pair, offset)
        grad_query = grad_query + query_part
        carried = from_behind(carried + key_part, "seq", -1)
        if offset > 1:
            kv_pair = from_behind(kv_pair, "seq", -1)
    carried = carried + own_part
    summed = lax.psum_scatter(carried, "head", scatter_dimension=1, tiled=True)
    grad_key = summed[0].astype(jnp.bfloat16)
    grad_value = summed[1].astype(jnp.bfloat16)
    return (
        grad_query.reshape(extent, local_heads * head_dim).astype(jnp.bfloat16),
        grad_key,
        grad_value,
    )


def solution(mesh):
    placed = (
        P("seq", "head"),
        P("seq", None),
        P("seq", None),
        P("seq", "head"),
        P("seq", "head"),
        P("head", "seq"),
        P(),
    )
    return jax.shard_map(
        shards,
        mesh=mesh,
        in_specs=placed,
        out_specs=(P("seq", "head"), P(("seq", "head"), None), P(("seq", "head"), None)),
        check_vma=False,
    )
```

profile of v0, /device:TPU:0, one launch (start us, length us, event | category | flops | bytes accessed | tf_op | source)
XLA Modules:
  0.0 166.5 jit_solution(5302465309677904088)
XLA Ops:
  8.3 3.5 %collective-permute-start = (bf16[2,512,128]{2,1,0:T(8,128)(2,1)S(1)}, bf16[2,512,128]{2,1,0:T(8,128)(2,1)S(1)}, u32[]{:S(2)}, u32[]{:S(2)}) collective-permute-start(bf16[2,512,128]{2,1,0:T(8,128)(2,1)S(1)} %pad_maximum_fusion.1), channel_id=1, source_target_pairs={{18,0},{20,2},{22,4},{24,6},{26,8},{28,10},{30,12},{0,14},{2,16},{... | collective-permute-start | bytes 786440 | tf_op jit(solution)/shard_map/ppermute | solution.py:12
  30.0 1.6 fusion.29
  34.6 1.7 fusion.25
  37.0 2.7 %collective-permute-start.7 = (f32[2,512,128]{2,1,0:T(8,128)S(1)}, f32[2,512,128]{2,1,0:T(8,128)S(1)}, u32[]{:S(2)}, u32[]{:S(2)}) collective-permute-start(f32[2,512,128]{2,1,0:T(8,128)S(1)} %pad_maximum_fusion), channel_id=1, source_target_pairs={{2,0},{4,2},{6,4},{8,6},{10,8},{12,10},{14,12},{16,14},{18,16},{20... | collective-permute-start | bytes 1572872 | tf_op jit(solution)/shard_map/ppermute | solution.py:12
  40.4 8.8 %collective-permute-done.1 = bf16[2,512,128]{2,1,0:T(8,128)(2,1)S(1)} collective-permute-done((bf16[2,512,128]{2,1,0:T(8,128)(2,1)S(1)}, bf16[2,512,128]{2,1,0:T(8,128)(2,1)S(1)}, u32[]{:S(2)}, u32[]{:S(2)}) %collective-permute-start.1) | collective-permute-done | bytes 262176 | tf_op jit(solution)/shard_map/ppermute | solution.py:12
  49.9 4.8 %collective-permute-start.2 = (bf16[2,512,128]{2,1,0:T(8,128)(2,1)S(1)}, bf16[2,512,128]{2,1,0:T(8,128)(2,1)S(1)}, u32[]{:S(2)}, u32[]{:S(2)}) collective-permute-start(bf16[2,512,128]{2,1,0:T(8,128)(2,1)S(1)} %collective-permute-done.1), channel_id=1, source_target_pairs={{2,0},{4,2},{6,4},{8,6},{10,8},{12,10},{14,12},{16,14},{18,16},{20... | collective-permute-start | bytes 786440 | tf_op jit(solution)/shard_map/ppermute | solution.py:12
  54.7 1.6 fusion.21
  61.9 4.7 %collective-permute-start.3 = (bf16[2,512,128]{2,1,0:T(8,128)(2,1)S(1)}, bf16[2,512,128]{2,1,0:T(8,128)(2,1)S(1)}, u32[]{:S(2)}, u32[]{:S(2)}) collective-permute-start(bf16[2,512,128]{2,1,0:T(8,128)(2,1)S(1)} %collective-permute-done.2), channel_id=1, source_target_pairs={{2,0},{4,2},{6,4},{8,6},{10,8},{12,10},{14,12},{16,14},{18,16},{20... | collective-permute-start | bytes 786440 | tf_op jit(solution)/shard_map/ppermute | solution.py:12
  67.3 3.2 %collective-permute-done.3 = bf16[2,512,128]{2,1,0:T(8,128)(2,1)S(1)} collective-permute-done((bf16[2,512,128]{2,1,0:T(8,128)(2,1)S(1)}, bf16[2,512,128]{2,1,0:T(8,128)(2,1)S(1)}, u32[]{:S(2)}, u32[]{:S(2)}) %collective-permute-start.3) | collective-permute-done | bytes 262176 | tf_op jit(solution)/shard_map/ppermute | solution.py:12
  71.2 4.7 %collective-permute-start.4 = (bf16[2,512,128]{2,1,0:T(8,128)(2,1)S(1)}, bf16[2,512,128]{2,1,0:T(8,128)(2,1)S(1)}, u32[]{:S(2)}, u32[]{:S(2)}) collective-permute-start(bf16[2,512,128]{2,1,0:T(8,128)(2,1)S(1)} %collective-permute-done.3), channel_id=1, source_target_pairs={{2,0},{4,2},{6,4},{8,6},{10,8},{12,10},{14,12},{16,14},{18,16},{20... | collective-permute-start | bytes 786440 | tf_op jit(solution)/shard_map/ppermute | solution.py:12
  81.4 1.6 fusion.9
  83.1 4.7 %collective-permute-start.5 = (bf16[2,512,128]{2,1,0:T(8,128)(2,1)S(1)}, bf16[2,512,128]{2,1,0:T(8,128)(2,1)S(1)}, u32[]{:S(2)}, u32[]{:S(2)}) collective-permute-start(bf16[2,512,128]{2,1,0:T(8,128)(2,1)S(1)} %collective-permute-done.4), channel_id=1, source_target_pairs={{2,0},{4,2},{6,4},{8,6},{10,8},{12,10},{14,12},{16,14},{18,16},{20... | collective-permute-start | bytes 786440 | tf_op jit(solution)/shard_map/ppermute | solution.py:12
  88.4 3.2 %collective-permute-done.5 = bf16[2,512,128]{2,1,0:T(8,128)(2,1)S(1)} collective-permute-done((bf16[2,512,128]{2,1,0:T(8,128)(2,1)S(1)}, bf16[2,512,128]{2,1,0:T(8,128)(2,1)S(1)}, u32[]{:S(2)}, u32[]{:S(2)}) %collective-permute-start.5) | collective-permute-done | bytes 262176 | tf_op jit(solution)/shard_map/ppermute | solution.py:12
  92.3 4.7 %collective-permute-start.6 = (bf16[2,512,128]{2,1,0:T(8,128)(2,1)S(1)}, bf16[2,512,128]{2,1,0:T(8,128)(2,1)S(1)}, u32[]{:S(2)}, u32[]{:S(2)}) collective-permute-start(bf16[2,512,128]{2,1,0:T(8,128)(2,1)S(1)} %collective-permute-done.5), channel_id=1, source_target_pairs={{2,0},{4,2},{6,4},{8,6},{10,8},{12,10},{14,12},{16,14},{18,16},{20... | collective-permute-start | bytes 786440 | tf_op jit(solution)/shard_map/ppermute | solution.py:12
  100.6 5.8 %collective-permute-done.10 = f32[2,512,128]{2,1,0:T(8,128)S(1)} collective-permute-done((f32[2,512,128]{2,1,0:T(8,128)S(1)}, f32[2,512,128]{2,1,0:T(8,128)S(1)}, u32[]{:S(2)}, u32[]{:S(2)}) %collective-permute-start.10) | collective-permute-done | bytes 524320 | tf_op jit(solution)/shard_map/ppermute | solution.py:12
  106.5 4.7 %collective-permute-start.11 = (f32[2,512,128]{2,1,0:T(8,128)S(1)}, f32[2,512,128]{2,1,0:T(8,128)S(1)}, u32[]{:S(2)}, u32[]{:S(2)}) collective-permute-start(f32[2,512,128]{2,1,0:T(8,128)S(1)} %maximum_add_fusion.3), channel_id=1, source_target_pairs={{2,0},{4,2},{6,4},{8,6},{10,8},{12,10},{14,12},{16,14},{18,16},{20... | collective-permute-start | bytes 1572872 | tf_op jit(solution)/shard_map/ppermute | solution.py:12
  111.9 1.7 fusion.1
  113.6 4.3 %collective-permute-done.11 = f32[2,512,128]{2,1,0:T(8,128)S(1)} collective-permute-done((f32[2,512,128]{2,1,0:T(8,128)S(1)}, f32[2,512,128]{2,1,0:T(8,128)S(1)}, u32[]{:S(2)}, u32[]{:S(2)}) %collective-permute-start.11) | collective-permute-done | bytes 524320 | tf_op jit(solution)/shard_map/ppermute | solution.py:12
  117.9 4.7 %collective-permute-start.12 = (f32[2,512,128]{2,1,0:T(8,128)S(1)}, f32[2,512,128]{2,1,0:T(8,128)S(1)}, u32[]{:S(2)}, u32[]{:S(2)}) collective-permute-start(f32[2,512,128]{2,1,0:T(8,128)S(1)} %maximum_add_fusion.4), channel_id=1, source_target_pairs={{2,0},{4,2},{6,4},{8,6},{10,8},{12,10},{14,12},{16,14},{18,16},{20... | collective-permute-start | bytes 1572872 | tf_op jit(solution)/shard_map/ppermute | solution.py:12
  124.3 5.0 %collective-permute-done.12 = f32[2,512,128]{2,1,0:T(8,128)S(1)} collective-permute-done((f32[2,512,128]{2,1,0:T(8,128)S(1)}, f32[2,512,128]{2,1,0:T(8,128)S(1)}, u32[]{:S(2)}, u32[]{:S(2)}) %collective-permute-start.12) | collective-permute-done | bytes 524320 | tf_op jit(solution)/shard_map/ppermute | solution.py:12
  129.4 4.9 %collective-permute-start.13 = (f32[2,512,128]{2,1,0:T(8,128)S(1)}, f32[2,512,128]{2,1,0:T(8,128)S(1)}, u32[]{:S(2)}, u32[]{:S(2)}) collective-permute-start(f32[2,512,128]{2,1,0:T(8,128)S(1)} %maximum_add_fusion.5), channel_id=1, source_target_pairs={{2,0},{4,2},{6,4},{8,6},{10,8},{12,10},{14,12},{16,14},{18,16},{20... | collective-permute-start | bytes 1572872 | tf_op jit(solution)/shard_map/ppermute | solution.py:12
  135.2 5.8 %collective-permute-done.13 = f32[2,512,128]{2,1,0:T(8,128)S(1)} collective-permute-done((f32[2,512,128]{2,1,0:T(8,128)S(1)}, f32[2,512,128]{2,1,0:T(8,128)S(1)}, u32[]{:S(2)}, u32[]{:S(2)}) %collective-permute-start.13) | collective-permute-done | bytes 524320 | tf_op jit(solution)/shard_map/ppermute | solution.py:12
  141.9 2.2 %fusion.67 = f32[512,4,128]{0,2,1:T(8,128)S(1)} fusion(f32[512,4,128]{0,2,1:T(8,128)S(1)} %fusion.68, bf16[4,512,512]{1,2,0:T(8,128)(2,1)} %copy-done.1, bf16[2,512,128]{2,1,0:T(8,128)(2,1)S(1)} %collective-permute-done.3), kind=kOutput, calls=%fused_computation.79 | convolution fusion | flops 268697600 | bytes 4325376 | tf_op jit(solution)/shard_map/hst,td->shd/dot_general | solution.py:36
  147.4 10.7 %reduce-scatter.2.cloned.1.call-done = f32[2,256,128]{2,1,0:T(8,128)} async-done(((f32[2,512,128]{2,1,0:T(8,128)}), f32[2,256,128]{2,1,0:T(8,128)}) %reduce-scatter.2.cloned.1.call-update) | async-done | bytes 262160 | tf_op jit(solution)/shard_map/reduce_scatter | solution.py:83
  (98 shorter events, 40.7 us)
Async XLA Ops:
  7.2 21.1 %copy-start = (bf16[512,512]{1,0:T(8,128)(2,1)S(1)}, bf16[512,512]{1,0:T(8,128)(2,1)}, u32[]{:S(2)}) copy-start(bf16[512,512]{1,0:T(8,128)(2,1)} %param.7) | copy-start | bytes 1572868
  7.2 21.1 %copy-start.8 = (bf16[512,128]{1,0:T(8,128)(2,1)S(1)}, bf16[512,128]{1,0:T(8,128)(2,1)}, u32[]{:S(2)}) copy-start(bf16[512,128]{1,0:T(8,128)(2,1)} %param.8) | copy-start | bytes 393220
  7.2 150.9 %reduce-scatter.2.cloned.1.call-start = ((), (), s32[]{:S(2)}) async-start(), calls=%async_computation.1 | async-start | bytes 786432 | tf_op jit(solution)/shard_map/reduce_scatter | solution.py:83
  8.3 24.6 %collective-permute-start = (bf16[2,512,128]{2,1,0:T(8,128)(2,1)S(1)}, bf16[2,512,128]{2,1,0:T(8,128)(2,1)S(1)}, u32[]{:S(2)}, u32[]{:S(2)}) collective-permute-start(bf16[2,512,128]{2,1,0:T(8,128)(2,1)S(1)} %pad_maximum_fusion.1), channel_id=1, source_target_pairs={{18,0},{20,2},{22,4},{24,6},{26,8},{28,10},{30,12},{0,14},{2,16},{... | collective-permute-start | bytes 786440 | tf_op jit(solution)/shard_map/ppermute | solution.py:12
  17.9 11.2 %copy-start.9 = (bf16[512,512]{1,0:T(8,128)(2,1)S(1)}, bf16[512,512]{1,0:T(8,128)(2,1)}, u32[]{:S(2)}) copy-start(bf16[512,512]{1,0:T(8,128)(2,1)} %param.11) | copy-start | bytes 1572868
  17.9 11.2 %copy-start.12 = (f32[4,512]{1,0:T(4,128)S(1)}, f32[4,512]{1,0:T(4,128)}, u32[]{:S(2)}) copy-start(f32[4,512]{1,0:T(4,128)} %param.12) | copy-start | bytes 24580
  37.0 21.1 %collective-permute-start.7 = (f32[2,512,128]{2,1,0:T(8,128)S(1)}, f32[2,512,128]{2,1,0:T(8,128)S(1)}, u32[]{:S(2)}, u32[]{:S(2)}) collective-permute-start(f32[2,512,128]{2,1,0:T(8,128)S(1)} %pad_maximum_fusion), channel_id=1, source_target_pairs={{2,0},{4,2},{6,4},{8,6},{10,8},{12,10},{14,12},{16,14},{18,16},{20... | collective-permute-start | bytes 1572872 | tf_op jit(solution)/shard_map/ppermute | solution.py:12
  39.7 9.5 %collective-permute-start.1 = (bf16[2,512,128]{2,1,0:T(8,128)(2,1)S(1)}, bf16[2,512,128]{2,1,0:T(8,128)(2,1)S(1)}, u32[]{:S(2)}, u32[]{:S(2)}) collective-permute-start(bf16[2,512,128]{2,1,0:T(8,128)(2,1)S(1)} %collective-permute-done), channel_id=1, source_target_pairs={{2,0},{4,2},{6,4},{8,6},{10,8},{12,10},{14,12},{16,14},{18,16},{20... | collective-permute-start | bytes 786440 | tf_op jit(solution)/shard_map/ppermute | solution.py:12
  49.9 8.7 %collective-permute-start.2 = (bf16[2,512,128]{2,1,0:T(8,128)(2,1)S(1)}, bf16[2,512,128]{2,1,0:T(8,128)(2,1)S(1)}, u32[]{:S(2)}, u32[]{:S(2)}) collective-permute-start(bf16[2,512,128]{2,1,0:T(8,128)(2,1)S(1)} %collective-permute-done.1), channel_id=1, source_target_pairs={{2,0},{4,2},{6,4},{8,6},{10,8},{12,10},{14,12},{16,14},{18,16},{20... | collective-permute-start | bytes 786440 | tf_op jit(solution)/shard_map/ppermute | solution.py:12
  58.1 21.0 %collective-permute-start.8 = (f32[2,512,128]{2,1,0:T(8,128)S(1)}, f32[2,512,128]{2,1,0:T(8,128)S(1)}, u32[]{:S(2)}, u32[]{:S(2)}) collective-permute-start(f32[2,512,128]{2,1,0:T(8,128)S(1)} %maximum_add_fusion), channel_id=1, source_target_pairs={{2,0},{4,2},{6,4},{8,6},{10,8},{12,10},{14,12},{16,14},{18,16},{20... | collective-permute-start | bytes 1572872 | tf_op jit(solution)/shard_map/ppermute | solution.py:12
  61.9 8.6 %collective-permute-start.3 = (bf16[2,512,128]{2,1,0:T(8,128)(2,1)S(1)}, bf16[2,512,128]{2,1,0:T(8,128)(2,1)S(1)}, u32[]{:S(2)}, u32[]{:S(2)}) collective-permute-start(bf16[2,512,128]{2,1,0:T(8,128)(2,1)S(1)} %collective-permute-done.2), channel_id=1, source_target_pairs={{2,0},{4,2},{6,4},{8,6},{10,8},{12,10},{14,12},{16,14},{18,16},{20... | collective-permute-start | bytes 786440 | tf_op jit(solution)/shard_map/ppermute | solution.py:12
  71.2 8.5 %collective-permute-start.4 = (bf16[2,512,128]{2,1,0:T(8,128)(2,1)S(1)}, bf16[2,512,128]{2,1,0:T(8,128)(2,1)S(1)}, u32[]{:S(2)}, u32[]{:S(2)}) collective-permute-start(bf16[2,512,128]{2,1,0:T(8,128)(2,1)S(1)} %collective-permute-done.3), channel_id=1, source_target_pairs={{2,0},{4,2},{6,4},{8,6},{10,8},{12,10},{14,12},{16,14},{18,16},{20... | collective-permute-start | bytes 786440 | tf_op jit(solution)/shard_map/ppermute | solution.py:12
  79.2 19.4 %collective-permute-start.9 = (f32[2,512,128]{2,1,0:T(8,128)S(1)}, f32[2,512,128]{2,1,0:T(8,128)S(1)}, u32[]{:S(2)}, u32[]{:S(2)}) collective-permute-start(f32[2,512,128]{2,1,0:T(8,128)S(1)} %maximum_add_fusion.1), channel_id=1, source_target_pairs={{2,0},{4,2},{6,4},{8,6},{10,8},{12,10},{14,12},{16,14},{18,16},{20... | collective-permute-start | bytes 1572872 | tf_op jit(solution)/shard_map/ppermute | solution.py:12
  83.0 15.6 %copy-start.2 = (bf16[4,512,512]{1,2,0:T(8,128)(2,1)}, bf16[4,512,512]{1,2,0:T(8,128)(2,1)S(1)}, u32[]{:S(2)}) copy-start(bf16[4,512,512]{1,2,0:T(8,128)(2,1)S(1)} %fusion.9) | copy-start | bytes 6291460
  83.1 8.5 %collective-permute-start.5 = (bf16[2,512,128]{2,1,0:T(8,128)(2,1)S(1)}, bf16[2,512,128]{2,1,0:T(8,128)(2,1)S(1)}, u32[]{:S(2)}, u32[]{:S(2)}) collective-permute-start(bf16[2,512,128]{2,1,0:T(8,128)(2,1)S(1)} %collective-permute-done.4), channel_id=1, source_target_pairs={{2,0},{4,2},{6,4},{8,6},{10,8},{12,10},{14,12},{16,14},{18,16},{20... | collective-permute-start | bytes 786440 | tf_op jit(solution)/shard_map/ppermute | solution.py:12
  92.3 18.9 %collective-permute-start.6 = (bf16[2,512,128]{2,1,0:T(8,128)(2,1)S(1)}, bf16[2,512,128]{2,1,0:T(8,128)(2,1)S(1)}, u32[]{:S(2)}, u32[]{:S(2)}) collective-permute-start(bf16[2,512,128]{2,1,0:T(8,128)(2,1)S(1)} %collective-permute-done.5), channel_id=1, source_target_pairs={{2,0},{4,2},{6,4},{8,6},{10,8},{12,10},{14,12},{16,14},{18,16},{20... | collective-permute-start | bytes 786440 | tf_op jit(solution)/shard_map/ppermute | solution.py:12
  98.7 7.8 %collective-permute-start.10 = (f32[2,512,128]{2,1,0:T(8,128)S(1)}, f32[2,512,128]{2,1,0:T(8,128)S(1)}, u32[]{:S(2)}, u32[]{:S(2)}) collective-permute-start(f32[2,512,128]{2,1,0:T(8,128)S(1)} %maximum_add_fusion.2), channel_id=1, source_target_pairs={{2,0},{4,2},{6,4},{8,6},{10,8},{12,10},{14,12},{16,14},{18,16},{20... | collective-permute-start | bytes 1572872 | tf_op jit(solution)/shard_map/ppermute | solution.py:12
  106.5 11.4 %collective-permute-start.11 = (f32[2,512,128]{2,1,0:T(8,128)S(1)}, f32[2,512,128]{2,1,0:T(8,128)S(1)}, u32[]{:S(2)}, u32[]{:S(2)}) collective-permute-start(f32[2,512,128]{2,1,0:T(8,128)S(1)} %maximum_add_fusion.3), channel_id=1, source_target_pairs={{2,0},{4,2},{6,4},{8,6},{10,8},{12,10},{14,12},{16,14},{18,16},{20... | collective-permute-start | bytes 1572872 | tf_op jit(solution)/shard_map/ppermute | solution.py:12
  113.6 10.7 %copy-start.6 = (bf16[4,512,512]{1,2,0:T(8,128)(2,1)}, bf16[4,512,512]{1,2,0:T(8,128)(2,1)S(1)}, u32[]{:S(2)}) copy-start(bf16[4,512,512]{1,2,0:T(8,128)(2,1)S(1)} %fusion.1) | copy-start | bytes 6291460
  117.9 11.4 %collective-permute-start.12 = (f32[2,512,128]{2,1,0:T(8,128)S(1)}, f32[2,512,128]{2,1,0:T(8,128)S(1)}, u32[]{:S(2)}, u32[]{:S(2)}) collective-permute-start(f32[2,512,128]{2,1,0:T(8,128)S(1)} %maximum_add_fusion.4), channel_id=1, source_target_pairs={{2,0},{4,2},{6,4},{8,6},{10,8},{12,10},{14,12},{16,14},{18,16},{20... | collective-permute-start | bytes 1572872 | tf_op jit(solution)/shard_map/ppermute | solution.py:12
  129.4 11.6 %collective-permute-start.13 = (f32[2,512,128]{2,1,0:T(8,128)S(1)}, f32[2,512,128]{2,1,0:T(8,128)S(1)}, u32[]{:S(2)}, u32[]{:S(2)}) collective-permute-start(f32[2,512,128]{2,1,0:T(8,128)S(1)} %maximum_add_fusion.5), channel_id=1, source_target_pairs={{2,0},{4,2},{6,4},{8,6},{10,8},{12,10},{14,12},{16,14},{18,16},{20... | collective-permute-start | bytes 1572872 | tf_op jit(solution)/shard_map/ppermute | solution.py:12
  141.9 2.2 %copy-start.3 = (bf16[4,512,512]{1,2,0:T(8,128)(2,1)S(1)}, bf16[4,512,512]{1,2,0:T(8,128)(2,1)}, u32[]{:S(2)}) copy-start(bf16[4,512,512]{1,2,0:T(8,128)(2,1)} %copy-done.2) | copy-start | bytes 6291460
  141.9 2.8 %copy-start.5 = (bf16[4,512,512]{1,2,0:T(8,128)(2,1)S(1)}, bf16[4,512,512]{1,2,0:T(8,128)(2,1)}, u32[]{:S(2)}) copy-start(bf16[4,512,512]{1,2,0:T(8,128)(2,1)} %copy-done.4) | copy-start | bytes 6291460
  144.2 1.7 %copy-start.7 = (bf16[4,512,512]{1,2,0:T(8,128)(2,1)S(1)}, bf16[4,512,512]{1,2,0:T(8,128)(2,1)}, u32[]{:S(2)}) copy-start(bf16[4,512,512]{1,2,0:T(8,128)(2,1)} %copy-done.6) | copy-start | bytes 6291460
  (4 other events, 5.4 us)
Sparse Core Ops, SparseCore 0:
  142.0 15.9 reduce-scatter.1
where the time goes:
time: 167 us
  waiting for transfers between devices  47.5 us (28%)
  starting transfers between devices  44.5 us (27%)
  matrix products  37.4 us (22%)
  between operations  24.7 us (15%)
  other arithmetic  7.03 us (4%)
  local copies, waits for them, and re-layouts  5.4 us (3%)
    ppermute x14, starting transfers between devices, from_behind(): return lax.ppermute(block, axis, route)  44.5 us
    ppermute x14, waiting for transfers between devices, from_behind(): return lax.ppermute(block, axis, route)  36.8 us
    dot_general x8, matrix products, block_terms(): jnp.einsum('shd,td->hst', grad_heads, value_block, preferred_element_type...  13.1 us
    reduce_scatter x1, waiting for transfers between devices, shards(): summed = lax.psum_scatter(carried, 'head', scatter_dimension=1, tiled=True)  10.7 us
    dot_general x8, matrix products, block_terms(): jnp.einsum('hst,shd->td', weights_low, grad_heads, preferred_element_type...  7.49 us
    dot_general x8, matrix products, block_terms(): jnp.einsum('shd,td->hst', query_heads, key_block, preferred_element_type=...  5.65 us
    dot_general x8, matrix products, block_terms(): jnp.einsum('hst,shd->td', grad_scores, query_heads, preferred_element_typ...  5.64 us
    dot_general x8, matrix products, block_terms(): jnp.einsum('hst,td->shd', grad_scores, key_block, preferred_element_type=...  5.5 us
  transfers between devices with their start and end apart: 15, of which 10 were waited for; matrix products, arithmetic and copies ran while one was open for 25% of the time, Pallas kernels for 0%

commit v1 on v0

v1 whole, which is shorter than its diff:
```python
import functools

import jax
import jax.numpy as jnp
from jax import lax
from jax.experimental import pallas as pl
from jax.experimental.pallas import tpu as pltpu
from jax.sharding import PartitionSpec as P

WINDOW = 8
GROUP = WINDOW // 2
LOG2E = 1.4426950408889634
F32 = jnp.float32
BF16 = jnp.bfloat16
STEPS = ((0, 0), (1, 0), (1, 1), (1, 2), (1, 3), (0, 2), (0, 3), (0, 1))


def dot(a, b, ca, cb):
    return lax.dot_general(a, b, (((ca,), (cb,)), ((), ())), preferred_element_type=F32)


def kernel(
    n, stripe, q_hbm, k_hbm, v_hbm, o_hbm, g_hbm, lse_hbm,
    dq_out, dk_out, dv_out,
    q, g, o, lse, delta, kv, dqt, acc, part, rx, zs, fin,
    in_sem, kv_send, kv_recv, p_send, p_recv, z_send, z_recv,
):
    me = lax.axis_index("seq")
    y = lax.axis_index("head")
    j = lax.rem(me, GROUP)
    base = me - j
    S, D2 = kv.shape[1:]
    D = D2 // 2
    H = q.shape[1] // D
    half = S // 2
    factor = D ** -0.5

    def mate(t):
        low = j % 2
        high = j // 2
        low = (1 - low) if t & 1 else low
        high = (1 - high) if t & 2 else high
        return high * 2 + low

    def at(t):
        return base + mate(t)

    def plane(d):
        return lax.rem(me + d * GROUP + n, n)

    loads = [
        pltpu.make_async_copy(k_hbm, kv.at[j, :, pl.ds(0, D)], in_sem.at[0]),
        pltpu.make_async_copy(v_hbm, kv.at[j, :, pl.ds(D, D)], in_sem.at[1]),
        pltpu.make_async_copy(q_hbm, q, in_sem.at[2]),
        pltpu.make_async_copy(g_hbm, g, in_sem.at[3]),
        pltpu.make_async_copy(o_hbm, o, in_sem.at[4]),
        pltpu.make_async_copy(lse_hbm, lse, in_sem.at[5]),
    ]
    for c in loads:
        c.start()

    barrier = pltpu.get_barrier_semaphore()
    peers = [(at(t), y) for t in (1, 2, 3)] + [(at(t), 1 - y) for t in range(4)]
    peers += [(plane(d), y) for d in (1, -1, 2, -2)]
    for p in peers:
        pl.semaphore_signal(barrier, inc=1, device_id=p, device_id_type=pl.DeviceIdType.MESH)
    loads[0].wait()
    loads[1].wait()
    pl.semaphore_wait(barrier, len(peers))

    A = lambda i: i
    B = lambda i: GROUP + i
    C = 2 * GROUP

    def remote(src, dst, ss, rs, to):
        return pltpu.make_async_remote_copy(
            src_ref=src, dst_ref=dst, send_sem=ss, recv_sem=rs,
            device_id=to, device_id_type=pl.DeviceIdType.MESH,
        )

    def kv_copy(src, dst, sem, to):
        return remote(kv.at[src], kv.at[dst], kv_send.at[sem], kv_recv.at[dst], (to, y))

    up_b = kv_copy(A(j), B(j), 0, plane(1))
    up_c = kv_copy(B(j), C, 1, plane(1))
    own = {t: kv_copy(A(j), A(j), 1 + t, at(t)) for t in (1, 2)}
    late = {t: kv_copy(C, A(j), 1 + t, at(t)) for t in (1, 2)}
    b_out = {t: kv_copy(B(j), B(j), 3 + t, at(t)) for t in (1, 2)}
    b_relay = kv_copy(B(mate(2)), B(mate(2)), 6, at(1))
    a_relay = kv_copy(A(mate(2)), A(mate(2)), 7, at(1))

    def kv_arrived(slot):
        kv_copy(slot, slot, 0, at(1)).wait_recv()

    up_b.start()
    for t in (1, 2):
        pl.when(mate(t) > j)(own[t].start)

    for c in loads[2:]:
        c.wait()

    ones = jnp.ones((8, D), BF16)
    for h in range(H):
        cols = slice(h * D, (h + 1) * D)
        prod = g[:, cols].astype(F32) * o[:, cols].astype(F32)
        hi = prod.astype(BF16)
        rest = prod - hi.astype(F32)
        mid = rest.astype(BF16)
        low = (rest - mid.astype(F32)).astype(BF16)
        total = dot(ones, hi, 1, 1) + dot(ones, mid, 1, 1) + dot(ones, low, 1, 1)
        delta[h] = total
    dqt[...] = jnp.zeros_like(dqt)
    own_stripe = stripe[me]

    rows = lax.broadcasted_iota(jnp.int32, (half, half), 0)
    diff = lax.broadcasted_iota(jnp.int32, (half, half), 1) - rows

    def heads(slot, least, first):
        def one(h):
            cols = pl.ds(pl.multiple_of(h * D, D), D)
            k0, k1 = kv[slot, :half, :D], kv[slot, half:, :D]
            v0, v1 = kv[slot, :half, D:], kv[slot, half:, D:]
            qh, gh = q[:, cols], g[:, cols]
            l2 = lse[pl.ds(h, 1), :] * LOG2E
            dl = delta[h, 0:1, :]
            s0 = dot(k0, qh, 1, 1)
            s1 = dot(k1, qh[half:], 1, 1)
            w0 = dot(v0, gh, 1, 1)
            w1 = dot(v1, gh[half:], 1, 1)
            p0 = jnp.exp2(s0 * (factor * LOG2E) - l2)
            open_ = diff >= least
            p0 = jnp.concatenate([jnp.where(open_, p0[:, :half], 0.0), p0[:, half:]], axis=1)
            p1 = jnp.where(open_, jnp.exp2(s1 * (factor * LOG2E) - l2[:, half:]), 0.0)
            d0 = (p0 * (w0 - dl)).astype(BF16)
            d1 = (p1 * (w1 - dl[:, half:])).astype(BF16)
            dv0 = dot(p0.astype(BF16), gh, 1, 0)
            dv1 = dot(p1.astype(BF16), gh[half:], 1, 0)
            dk0 = dot(d0, qh, 1, 0)
            dk1 = dot(d1, qh[half:], 1, 0)
            dqt[h, :, :] += dot(k0, d0, 0, 0)
            dqt[h, :, half:] += dot(k1, d1, 0, 0)
            return dk0, dv0, dk1, dv1

        return one

    def compute(slot, late_flag, i, between):
        if late_flag:
            source = base - GROUP + i
        else:
            source = base + i - jnp.where(i > j, 2 * GROUP, 0)
        source = lax.rem(source + n, n)
        least = jnp.where(stripe[source] <= own_stripe, 0, 1)
        one = heads(slot, least, True)

        def pair(h0, keep):
            a = one(h0)
            b = one(h0 + 1)
            for m in range(4):
                r, c = m // 2, m % 2
                s = a[m] + b[m]
                if keep:
                    s = s + acc[r, :, c * D:(c + 1) * D]
                acc[r, :, c * D:(c + 1) * D] = s

        pair(0, False)
        between()

        @pl.loop(1, H // 2)
        def _(m):
            pair(2 * m, True)

    def part_copies(step):
        late_flag, t = STEPS[step]
        to = at(t)
        res = []
        if t:
            res.append(remote(part.at[step, y], rx.at[late_flag, t, 0],
                              p_send.at[step, 0], p_recv.at[late_flag, t, 0], (to, y)))
        res.append(remote(part.at[step, 1 - y], rx.at[late_flag, t, 1],
                          p_send.at[step, 1], p_recv.at[late_flag, t, 1], (to, 1 - y)))
        return res

    def send_part(step):
        for c in part_copies(step):
            c.start()

    z_copies = [
        remote(zs.at[m], fin.at[m], z_send.at[m], z_recv.at[m], (plane(-1 - m), y)) for m in range(2)
    ]
    bsteps = {t: STEPS.index((1, t)) for t in range(4)}
    asteps = {t: STEPS.index((0, t)) for t in range(4)}

    def arrived_part(flag, t):
        def get(m):
            remote(rx.at[flag, t, m], rx.at[flag, t, m], p_send.at[0, 0], p_recv.at[flag, t, m],
                   (at(1), y)).wait_recv()
            return rx[flag, t, m].astype(F32)

        first = part[STEPS.index((flag, 0)), y].astype(F32) if t == 0 else get(0)
        return first + get(1)

    for step, (flag, t) in enumerate(STEPS):
        i = mate(t)
        slot = B(i) if flag else A(i)
        if (flag, t) == (1, 0):
            kv_arrived(slot)
            up_c.start()
            b_out[1].start()
            b_out[2].start()
        elif (flag, t) == (1, 2):
            kv_arrived(slot)
            b_relay.start()
            kv_arrived(C)
            for u in (1, 2):
                pl.when(mate(u) < j)(late[u].start)
        elif (flag, t) == (0, 2):
            kv_arrived(slot)
            a_relay.start()
        elif (flag, t) != (0, 0):
            kv_arrived(slot)

        def between():
            if step:
                send_part(step - 1)

        compute(slot, flag, i, between)
        for r in range(2):
            part[step, r] = acc[r].astype(BF16)
        if step == 6:
            total = arrived_part(1, 0)
            for u in (1, 2, 3):
                total = total + arrived_part(1, u)
            zs[0] = total.astype(BF16)

    send_part(len(STEPS) - 1)
    z_copies[0].start()

    for h in range(H):
        dq_out[:, h * D:(h + 1) * D] = (dqt[h] * factor).T.astype(BF16)

    mine = arrived_part(0, 0)
    other = jnp.zeros_like(mine)
    for u in (2, 3, 1):
        x = arrived_part(0, u)
        here = mate(u) > j
        mine = mine + jnp.where(here, x, 0.0)
        other = other + jnp.where(here, 0.0, x)
    zs[1] = other.astype(BF16)
    z_copies[1].start()
    z_copies[0].wait_recv()
    mine = mine + fin[0].astype(F32)
    z_copies[1].wait_recv()
    mine = mine + fin[1].astype(F32)
    dk_out[...] = (mine[:, :D] * factor).astype(BF16)
    dv_out[...] = mine[:, D:].astype(BF16)

    for c in [up_b, up_c, own[1], own[2], b_out[1], b_out[2], b_relay, a_relay]:
        c.wait_send()
    for step in range(len(STEPS)):
        for c in part_copies(step):
            c.wait_send()
    for c in z_copies:
        c.wait_send()


def shards(n, query, key_rows, value_rows, output, grad_output, log_norm, stripe):
    S, W = query.shape
    D = key_rows.shape[1]
    H = W // D
    half = S // 2
    any_ = pl.BlockSpec(memory_space=pl.ANY)
    vm = pl.BlockSpec(memory_space=pltpu.VMEM)
    dma = pltpu.SemaphoreType.DMA
    return pl.pallas_call(
        functools.partial(kernel, n),
        out_shape=(
            jax.ShapeDtypeStruct((S, W), BF16),
            jax.ShapeDtypeStruct((half, D), BF16),
            jax.ShapeDtypeStruct((half, D), BF16),
        ),
        in_specs=[pl.BlockSpec(memory_space=pltpu.SMEM)] + [any_] * 6,
        out_specs=(vm, vm, vm),
        scratch_shapes=[
            pltpu.VMEM((S, W), BF16),
            pltpu.VMEM((S, W), BF16),
            pltpu.VMEM((S, W), BF16),
            pltpu.VMEM((H, S), F32),
            pltpu.VMEM((H, 8, S), F32),
            pltpu.VMEM((2 * GROUP + 1, S, 2 * D), BF16),
            pltpu.VMEM((H, D, S), F32),
            pltpu.VMEM((2, half, 2 * D), F32),
            pltpu.VMEM((len(STEPS), 2, half, 2 * D), BF16),
            pltpu.VMEM((2, GROUP, 2, half, 2 * D), BF16),
            pltpu.VMEM((2, half, 2 * D), BF16),
            pltpu.VMEM((2, half, 2 * D), BF16),
            dma((6,)),
            dma((8,)),
            dma((2 * GROUP + 1,)),
            dma((len(STEPS), 2)),
            dma((2, GROUP, 2)),
            dma((2,)),
            dma((2,)),
        ],
        compiler_params=pltpu.CompilerParams(
            collective_id=0, has_side_effects=True, vmem_limit_bytes=48 * 1024 * 1024
        ),
        name="window_backward",
    )(stripe, query, key_rows, value_rows, output, grad_output, log_norm)


def solution(mesh):
    placed = (
        P("seq", "head"),
        P("seq", None),
        P("seq", None),
        P("seq", "head"),
        P("seq", "head"),
        P("head", "seq"),
        P(),
    )
    return jax.shard_map(
        functools.partial(shards, mesh.shape["seq"]),
        mesh=mesh,
        in_specs=placed,
        out_specs=(P("seq", "head"), P(("seq", "head"), None), P(("seq", "head"), None)),
        check_vma=False,
    )
```

time: 167 us -> 65.3 us (0.39)
  Pallas kernels: 0 us -> 55.8 us
  waiting for transfers between devices: 47.5 us -> 0 us
  starting transfers between devices: 44.5 us -> 0 us
  matrix products: 37.4 us -> 0 us
  between operations: 24.7 us -> 0.66 us
  other arithmetic: 7.03 us -> 0 us
  local copies, waits for them, and re-layouts: 5.4 us -> 8.33 us
    pallas_call x0 -> x1, Pallas kernels: none -> 55.8 us  [shards(): pl.pallas_call(functools.partial(kernel, n), out_shape=(jax.ShapeDtypeStr...]
    ppermute x14 -> x0, starting transfers between devices: 44.5 us -> none  [from_behind(): return lax.ppermute(block, axis, route)]
    dot_general x40 -> x0, matrix products: 37.4 us -> none  [the longest x8 13.1 us: block_terms(): jnp.einsum('shd,td->hst', grad_heads, value_block, preferred_element_type...]
    ppermute x14 -> x0, waiting for transfers between devices: 36.8 us -> none  [from_behind(): return lax.ppermute(block, axis, route)]
    reduce_scatter x1 -> x0, waiting for transfers between devices: 10.7 us -> none  [shards(): summed = lax.psum_scatter(carried, 'head', scatter_dimension=1, tiled=True)]
    unnamed x27 -> x17, local copies, waits for them, and re-layouts: 2.09 us -> 8.33 us
    reduce_sum x2 -> x0, other arithmetic: 2.09 us -> none  [the longest x1 1.47 us: stripe_at(): return jnp.sum(jnp.where(slot_ids == where_index, stripe, 0))]
    another operation x3 -> x0, other arithmetic: 2.05 us -> none  [the longest x1 1.05 us: shards(): kv_pair = jnp.stack([key_rows, value_rows])]
  transfers between devices with their start and end apart: 15 -> 0, of which waited for: 10 -> 0; matrix products, arithmetic and copies ran while one was open for 25% -> 0% of each run, Pallas kernels for 0% -> 0%
where the time goes in v1:
time: 65.3 us; the launch traced here: 64.8 us
  Pallas kernels  55.8 us (85%)
  local copies, waits for them, and re-layouts  8.33 us (13%)
  between operations  0.66 us (1%)
    pallas_call x1, Pallas kernels, shards(): pl.pallas_call(functools.partial(kernel, n), out_shape=(jax.ShapeDtypeStr...  55.8 us
    unnamed x17, local copies, waits for them, and re-layouts  8.33 us

profile of v1, /device:TPU:0, one launch (start us, length us, event | category | flops | bytes accessed | tf_op | source)
XLA Modules:
  0.0 64.8 jit_solution(15168411689676314117)
XLA Ops:
  0.6 0.0 copy-start
  0.6 1.0 %copy-done = bf16[512,512]{1,0:T(8,128)(2,1)S(1)} copy-done((bf16[512,512]{1,0:T(8,128)(2,1)S(1)}, bf16[512,512]{1,0:T(8,128)(2,1)}, u32[]{:S(2)}) %copy-start) | copy-done | bytes 524312
  1.7 0.0 copy-start.1
  1.7 1.0 %copy-done.1 = bf16[512,512]{1,0:T(8,128)(2,1)S(1)} copy-done((bf16[512,512]{1,0:T(8,128)(2,1)S(1)}, bf16[512,512]{1,0:T(8,128)(2,1)}, u32[]{:S(2)}) %copy-start.1) | copy-done | bytes 524312
  2.7 0.0 copy-start.2
  2.7 1.0 %copy-done.2 = bf16[512,512]{1,0:T(8,128)(2,1)S(1)} copy-done((bf16[512,512]{1,0:T(8,128)(2,1)S(1)}, bf16[512,512]{1,0:T(8,128)(2,1)}, u32[]{:S(2)}) %copy-start.2) | copy-done | bytes 524312
  3.8 0.0 copy-start.3
  3.8 0.9 %copy-done.3 = bf16[512,128]{1,0:T(8,128)(2,1)S(1)} copy-done((bf16[512,128]{1,0:T(8,128)(2,1)S(1)}, bf16[512,128]{1,0:T(8,128)(2,1)}, u32[]{:S(2)}) %copy-start.3) | copy-done | bytes 131096
  4.7 0.0 copy-start.4
  4.7 0.9 %copy-done.4 = bf16[512,128]{1,0:T(8,128)(2,1)S(1)} copy-done((bf16[512,128]{1,0:T(8,128)(2,1)S(1)}, bf16[512,128]{1,0:T(8,128)(2,1)}, u32[]{:S(2)}) %copy-start.4) | copy-done | bytes 131096
  5.6 0.0 copy-start.5
  5.6 0.7 %copy-done.5 = f32[4,512]{1,0:T(4,128)S(1)} copy-done((f32[4,512]{1,0:T(4,128)S(1)}, f32[4,512]{1,0:T(4,128)}, u32[]{:S(2)}) %copy-start.5) | copy-done | bytes 8216
  6.3 0.0 copy-start.6
  6.3 0.7 %copy-done.6 = s32[16]{0:T(128)S(1)} copy-done((s32[16]{0:T(128)S(1)}, s32[16]{0:T(128)}, u32[]{:S(2)}) %copy-start.6) | copy-done | bytes 88
  6.9 55.8 %window_backward.1 = (bf16[512,512]{1,0:T(8,128)(2,1)S(1)}, bf16[256,128]{1,0:T(8,128)(2,1)S(1)}, bf16[256,128]{1,0:T(8,128)(2,1)S(1)}) custom-call(s32[16]{0:T(128)S(1)} %copy-done.6, bf16[512,512]{1,0:T(8,128)(2,1)S(1)} %copy-done, bf16[512,128]{1,0:T(8,128)(2,1)S(1)} %copy-done.3, bf16[512,128]{1,0:T(8,128)(2,1)S(1)} %copy-done.4, ...), custom_call_target="tpu_custom_call" | custom-call | tf_op jit(solution)/shard_map/window_backward/pallas_call | solution.py:274
  62.7 0.8 %copy.13 = bf16[512,512]{1,0:T(8,128)(2,1)} copy(bf16[512,512]{1,0:T(8,128)(2,1)S(1)} %get-tuple-element.6) | data formatting | bytes 1048576
  63.5 0.6 copy.14
  64.2 0.6 copy.15
Async XLA Ops:
  0.6 1.0 %copy-start = (bf16[512,512]{1,0:T(8,128)(2,1)S(1)}, bf16[512,512]{1,0:T(8,128)(2,1)}, u32[]{:S(2)}) copy-start(bf16[512,512]{1,0:T(8,128)(2,1)} %q_hbm.1) | copy-start | bytes 1572868
  1.7 1.0 %copy-start.1 = (bf16[512,512]{1,0:T(8,128)(2,1)S(1)}, bf16[512,512]{1,0:T(8,128)(2,1)}, u32[]{:S(2)}) copy-start(bf16[512,512]{1,0:T(8,128)(2,1)} %o_hbm.1) | copy-start | bytes 1572868
  2.7 1.0 %copy-start.2 = (bf16[512,512]{1,0:T(8,128)(2,1)S(1)}, bf16[512,512]{1,0:T(8,128)(2,1)}, u32[]{:S(2)}) copy-start(bf16[512,512]{1,0:T(8,128)(2,1)} %g_hbm.1) | copy-start | bytes 1572868
  3.8 0.9 %copy-start.3 = (bf16[512,128]{1,0:T(8,128)(2,1)S(1)}, bf16[512,128]{1,0:T(8,128)(2,1)}, u32[]{:S(2)}) copy-start(bf16[512,128]{1,0:T(8,128)(2,1)} %k_hbm.1) | copy-start | bytes 393220
  4.7 0.9 %copy-start.4 = (bf16[512,128]{1,0:T(8,128)(2,1)S(1)}, bf16[512,128]{1,0:T(8,128)(2,1)}, u32[]{:S(2)}) copy-start(bf16[512,128]{1,0:T(8,128)(2,1)} %v_hbm.1) | copy-start | bytes 393220
  5.6 0.7 %copy-start.5 = (f32[4,512]{1,0:T(4,128)S(1)}, f32[4,512]{1,0:T(4,128)}, u32[]{:S(2)}) copy-start(f32[4,512]{1,0:T(4,128)} %lse_hbm.1) | copy-start | bytes 24580
  6.3 0.7 %copy-start.6 = (s32[16]{0:T(128)S(1)}, s32[16]{0:T(128)}, u32[]{:S(2)}) copy-start(s32[16]{0:T(128)} %stripe.1) | copy-start | bytes 196

commit v2 on v1

--- a/solution.py
+++ b/solution.py
@@ -12,7 +12,10 @@
 LOG2E = 1.4426950408889634
 F32 = jnp.float32
 BF16 = jnp.bfloat16
-STEPS = ((0, 0), (1, 0), (1, 1), (1, 2), (1, 3), (0, 2), (0, 3), (0, 1))
+STEPS = ((0, 0), (1, 1), (1, 0), (1, 3), (1, 2), (0, 3), (0, 2), (0, 1))
+GIVEN = {(1, 1): 0, (1, 3): 1, (0, 3): 2}
+TAKEN = {(1, 0): 0, (1, 2): 1, (0, 2): 2}
+SENT = ((0, 0), (1, 0), (1, 2), (0, 2), (0, 1))
 
 
 def dot(a, b, ca, cb):
@@ -22,8 +25,8 @@
 def kernel(
     n, stripe, q_hbm, k_hbm, v_hbm, o_hbm, g_hbm, lse_hbm,
     dq_out, dk_out, dv_out,
-    q, g, o, lse, delta, kv, dqt, acc, part, rx, zs, fin,
-    in_sem, kv_send, kv_recv, p_send, p_recv, z_send, z_recv,
+    q, g, o, lse, delta, kv, dqt, acc, give, take, part, rx, zs, fin,
+    in_sem, kv_send, kv_recv, d_send, d_recv, p_send, p_recv, z_send, z_recv,
 ):
     me = lax.axis_index("seq")
     y = lax.axis_index("head")
@@ -108,7 +111,7 @@
         mid = rest.astype(BF16)
         low = (rest - mid.astype(F32)).astype(BF16)
         total = dot(ones, hi, 1, 1) + dot(ones, mid, 1, 1) + dot(ones, low, 1, 1)
-        delta[h] = total
+        delta[h] = total * factor
     dqt[...] = jnp.zeros_like(dqt)
     own_stripe = stripe[me]
 
@@ -131,8 +134,8 @@
             open_ = diff >= least
             p0 = jnp.concatenate([jnp.where(open_, p0[:, :half], 0.0), p0[:, half:]], axis=1)
             p1 = jnp.where(open_, jnp.exp2(s1 * (factor * LOG2E) - l2[:, half:]), 0.0)
-            d0 = (p0 * (w0 - dl)).astype(BF16)
-            d1 = (p1 * (w1 - dl[:, half:])).astype(BF16)
+            d0 = (p0 * (w0 * factor - dl)).astype(BF16)
+            d1 = (p1 * (w1 * factor - dl[:, half:])).astype(BF16)
             dv0 = dot(p0.astype(BF16), gh, 1, 0)
             dv1 = dot(p1.astype(BF16), gh[half:], 1, 0)
             dk0 = dot(d0, qh, 1, 0)
@@ -169,78 +172,93 @@
         def _(m):
             pair(2 * m, True)
 
-    def part_copies(step):
-        late_flag, t = STEPS[step]
+    def part_copies(key):
+        late_flag, t = key
         to = at(t)
+        slot = SENT.index(key)
         res = []
         if t:
-            res.append(remote(part.at[step, y], rx.at[late_flag, t, 0],
-                              p_send.at[step, 0], p_recv.at[late_flag, t, 0], (to, y)))
-        res.append(remote(part.at[step, 1 - y], rx.at[late_flag, t, 1],
-                          p_send.at[step, 1], p_recv.at[late_flag, t, 1], (to, 1 - y)))
+            res.append(remote(part.at[slot, y], rx.at[slot, 0],
+                              p_send.at[slot, 0], p_recv.at[slot, 0], (to, y)))
+        res.append(remote(part.at[slot, 1 - y], rx.at[slot, 1],
+                          p_send.at[slot, 1], p_recv.at[slot, 1], (to, 1 - y)))
         return res
 
-    def send_part(step):
-        for c in part_copies(step):
-            c.start()
+    def pair_copy(m):
+        return remote(give.at[m], take.at[m], d_send.at[m], d_recv.at[m], (at(1), y))
+
+    def send_part(key):
+        if key in GIVEN:
+            pair_copy(GIVEN[key]).start()
+        else:
+            for c in part_copies(key):
+                c.start()
 
     z_copies = [
         remote(zs.at[m], fin.at[m], z_send.at[m], z_recv.at[m], (plane(-1 - m), y)) for m in range(2)
     ]
-    bsteps = {t: STEPS.index((1, t)) for t in range(4)}
-    asteps = {t: STEPS.index((0, t)) for t in range(4)}
 
     def arrived_part(flag, t):
+        slot = SENT.index((flag, t))
+
         def get(m):
-            remote(rx.at[flag, t, m], rx.at[flag, t, m], p_send.at[0, 0], p_recv.at[flag, t, m],
+            remote(rx.at[slot, m], rx.at[slot, m], p_send.at[0, 0], p_recv.at[slot, m],
                    (at(1), y)).wait_recv()
-            return rx[flag, t, m].astype(F32)
-
-        first = part[STEPS.index((flag, 0)), y].astype(F32) if t == 0 else get(0)
+            return rx[slot, m].astype(F32)
+
+        first = part[slot, y].astype(F32) if t == 0 else get(0)
         return first + get(1)
 
     for step, (flag, t) in enumerate(STEPS):
         i = mate(t)
         slot = B(i) if flag else A(i)
-        if (flag, t) == (1, 0):
-            kv_arrived(slot)
+        if (flag, t) == (1, 1):
+            kv_arrived(B(j))
             up_c.start()
             b_out[1].start()
             b_out[2].start()
-        elif (flag, t) == (1, 2):
             kv_arrived(slot)
+        elif (flag, t) == (1, 3):
+            kv_arrived(B(mate(2)))
             b_relay.start()
             kv_arrived(C)
             for u in (1, 2):
                 pl.when(mate(u) < j)(late[u].start)
-        elif (flag, t) == (0, 2):
             kv_arrived(slot)
+        elif (flag, t) == (0, 3):
+            kv_arrived(A(mate(2)))
             a_relay.start()
-        elif (flag, t) != (0, 0):
+            kv_arrived(slot)
+        elif (flag, t) == (0, 1):
             kv_arrived(slot)
 
         def between():
             if step:
-                send_part(step - 1)
+                send_part(STEPS[step - 1])
+            if step == 7:
+                z_copies[0].start()
 
         compute(slot, flag, i, between)
-        for r in range(2):
-            part[step, r] = acc[r].astype(BF16)
+        key = (flag, t)
+        if key in GIVEN:
+            give[GIVEN[key]] = acc[...]
+        elif key in TAKEN:
+            m = TAKEN[key]
+            pair_copy(m).wait_recv()
+            part[SENT.index(key)] = (acc[...] + take[m]).astype(BF16)
+        else:
+            part[SENT.index(key)] = acc[...].astype(BF16)
         if step == 6:
-            total = arrived_part(1, 0)
-            for u in (1, 2, 3):
-                total = total + arrived_part(1, u)
-            zs[0] = total.astype(BF16)
-
-    send_part(len(STEPS) - 1)
-    z_copies[0].start()
+            zs[0] = (arrived_part(1, 0) + arrived_part(1, 2)).astype(BF16)
+
+    send_part(STEPS[-1])
 
     for h in range(H):
-        dq_out[:, h * D:(h + 1) * D] = (dqt[h] * factor).T.astype(BF16)
+        dq_out[:, h * D:(h + 1) * D] = dqt[h].T.astype(BF16)
 
     mine = arrived_part(0, 0)
     other = jnp.zeros_like(mine)
-    for u in (2, 3, 1):
+    for u in (2, 1):
         x = arrived_part(0, u)
         here = mate(u) > j
         mine = mine + jnp.where(here, x, 0.0)
@@ -251,14 +269,16 @@
     mine = mine + fin[0].astype(F32)
     z_copies[1].wait_recv()
     mine = mine + fin[1].astype(F32)
-    dk_out[...] = (mine[:, :D] * factor).astype(BF16)
+    dk_out[...] = mine[:, :D].astype(BF16)
     dv_out[...] = mine[:, D:].astype(BF16)
 
     for c in [up_b, up_c, own[1], own[2], b_out[1], b_out[2], b_relay, a_relay]:
         c.wait_send()
-    for step in range(len(STEPS)):
-        for c in part_copies(step):
+    for key in SENT:
+        for c in part_copies(key):
             c.wait_send()
+    for m in range(len(GIVEN)):
+        pair_copy(m).wait_send()
     for c in z_copies:
         c.wait_send()
 
@@ -289,20 +309,24 @@
             pltpu.VMEM((2 * GROUP + 1, S, 2 * D), BF16),
             pltpu.VMEM((H, D, S), F32),
             pltpu.VMEM((2, half, 2 * D), F32),
-            pltpu.VMEM((len(STEPS), 2, half, 2 * D), BF16),
-            pltpu.VMEM((2, GROUP, 2, half, 2 * D), BF16),
+            pltpu.VMEM((len(GIVEN), 2, half, 2 * D), F32),
+            pltpu.VMEM((len(GIVEN), 2, half, 2 * D), F32),
+            pltpu.VMEM((len(SENT), 2, half, 2 * D), BF16),
+            pltpu.VMEM((len(SENT), 2, half, 2 * D), BF16),
             pltpu.VMEM((2, half, 2 * D), BF16),
             pltpu.VMEM((2, half, 2 * D), BF16),
             dma((6,)),
             dma((8,)),
             dma((2 * GROUP + 1,)),
-            dma((len(STEPS), 2)),
-            dma((2, GROUP, 2)),
+            dma((len(GIVEN),)),
+            dma((len(GIVEN),)),
+            dma((len(SENT), 2)),
+            dma((len(SENT), 2)),
             dma((2,)),
             dma((2,)),
         ],
         compiler_params=pltpu.CompilerParams(
-            collective_id=0, has_side_effects=True, vmem_limit_bytes=48 * 1024 * 1024
+            collective_id=0, has_side_effects=True, vmem_limit_bytes=67043328
         ),
         name="window_backward",
     )(stripe, query, key_rows, value_rows, output, grad_output, log_norm)

time: 65.3 us -> 60.7 us (0.930)
  local copies, waits for them, and re-layouts: 8.33 us -> 3.4 us
  Pallas kernels: 55.8 us -> 56.5 us
    unnamed x17 -> x7, local copies, waits for them, and re-layouts: 8.33 us -> 3.4 us
    pallas_call x1, Pallas kernels: 55.8 us -> 56.5 us  [shards(): pl.pallas_call(functools.partial(kernel, n), out_shape=(jax.ShapeDtypeStr...]
where the time goes in v2:
time: 60.7 us; the launch traced here: 60.5 us
  Pallas kernels  56.5 us (93%)
  local copies, waits for them, and re-layouts  3.4 us (6%)
  between operations  0.65 us (1%)
    pallas_call x1, Pallas kernels, shards(): pl.pallas_call(functools.partial(kernel, n), out_shape=(jax.ShapeDtypeStr...  56.5 us
    unnamed x7, local copies, waits for them, and re-layouts  3.4 us

profile of v2, /device:TPU:0, one launch (start us, length us, event | category | flops | bytes accessed | tf_op | source)
XLA Modules:
  0.0 60.5 jit_solution(668714728883872105)
XLA Ops:
  0.6 56.5 %window_backward.1 = (bf16[512,512]{1,0:T(8,128)(2,1)}, bf16[256,128]{1,0:T(8,128)(2,1)}, bf16[256,128]{1,0:T(8,128)(2,1)}) custom-call(s32[16]{0:T(128)} %stripe.1, bf16[512,512]{1,0:T(8,128)(2,1)} %q_hbm.1, bf16[512,128]{1,0:T(8,128)(2,1)} %k_hbm.1, bf16[512,128]{1,0:T(8,128)(2,1)} %v_hbm.1, bf16[512,512]{1,0:T(8,128)(2,1)} %o_hbm.1, ...), custom_call_target="tpu_custom_call" | custom-call | tf_op jit(solution)/shard_map/window_backward/pallas_call | solution.py:294
  57.1 0.0 copy-start.1
  57.1 1.9 %copy.13 = bf16[512,512]{1,0:T(8,128)(2,1)} copy(bf16[512,512]{1,0:T(8,128)(2,1)} %get-tuple-element.6) | data formatting | bytes 1048576
  59.0 0.0 copy-done.1
  59.0 0.0 copy-start
  59.0 0.6 %copy.14 = bf16[256,128]{1,0:T(8,128)(2,1)} copy(bf16[256,128]{1,0:T(8,128)(2,1)S(1)} %copy-done.1) | data formatting | bytes 131072
  59.7 0.2 copy-done
  59.9 0.6 %copy.15 = bf16[256,128]{1,0:T(8,128)(2,1)} copy(bf16[256,128]{1,0:T(8,128)(2,1)S(1)} %copy-done) | data formatting | bytes 131072
Async XLA Ops:
  57.1 1.9 %copy-start.1 = (bf16[256,128]{1,0:T(8,128)(2,1)S(1)}, bf16[256,128]{1,0:T(8,128)(2,1)}, u32[]{:S(2)}) copy-start(bf16[256,128]{1,0:T(8,128)(2,1)} %get-tuple-element.7) | copy-start | bytes 196612
  59.0 0.9 %copy-start = (bf16[256,128]{1,0:T(8,128)(2,1)S(1)}, bf16[256,128]{1,0:T(8,128)(2,1)}, u32[]{:S(2)}) copy-start(bf16[256,128]{1,0:T(8,128)(2,1)} %get-tuple-element.8) | copy-start | bytes 196612
